TPU v7x, 256 devices: a 8x8x2 block of a 8x8x16 slice. The times are simulated.
256 devices in a mesh: doc: 2 (over z), seq: 16 (over y, core), head: 8 (over x).
Axes of the slice: x: 8, y: 8, z: 2, core: 2. Of those that a mesh axis runs over, the one named last changes fastest.
The devices are a block of a 8x8x16 slice.
Arguments:
- length: int32 [2], P('doc'), parts along dimension 0, may hold values from 3968 to 4096
- residual: bfloat16 [8192, 4096], P(('doc', 'seq'), 'head'), parts along dimension 0, may hold values from -6 to 6
- ssm_input: bfloat16 [8192, 4096], P(('doc', 'seq'), 'head'), parts along dimension 0, may hold values from -6 to 6
- state_in: bfloat16 [8192, 128], P(('doc', 'seq')), parts along dimension 0, may hold values from -6 to 6
- state_out: bfloat16 [8192, 128], P(('doc', 'seq')), parts along dimension 0, may hold values from -0.5 to 0.5
- step_raw: float32 [128, 4096], P(('doc', 'head'), 'seq'), parts along dimension 0, may hold values from -5 to 2
- decay_rate: float32 [64], P('head'), may hold values from 0 to 1, as said below
- ssm_gain: float32 [4096], P('head'), may hold values from 0.1 to 1.9
- out_weight: bfloat16 [4096, 4096], P('head'), may hold values from -0.09375 to 0.09375
- norm_gain: float32 [4096], replicated, may hold values from 0.1 to 1.9
- query_weight: bfloat16 [4096, 4096], P(None, 'head'), may hold values from -2 to 2
- key_weight: bfloat16 [4096, 1024], P(None, 'head'), may hold values from -3 to 3
- value_weight: bfloat16 [4096, 1024], P(None, 'head'), may hold values from -0.09375 to 0.09375
Outputs:
- layer_out: bfloat16 [8192, 4096], P(('doc', 'seq'), 'head'), parts along dimension 0
- head_out: bfloat16 [8192, 4096], P(('doc', 'seq'), 'head'), parts along dimension 0
There are 2 independent parts, one for each index of `doc`. A program takes and returns all parts, laid end to end along the dimension named above; an argument that names none is the same for every part. Nothing has to cross between parts.
Inputs may be any that keep to these rules, and one draw needn't show every extreme that they name: The document fills positions 0 to length - 1 of the 4096; later positions are padding. `decay_rate`: positive.
All inputs are finite; a program needn't handle non-finite values.
Results may differ from a plain program's by a relative error of at most 0.028.
The roundings to bfloat16 on the way count: a program that leaves them out, or rounds other values in their place, can miss the bound.
Values may be sent and summed in bfloat16 or wider, within the bound.
A program may use at most 64 MiB of HBM per device.

v0:
```python
import jax
import jax.numpy as jnp
from jax import lax
from jax.sharding import Mesh
from jax.sharding import PartitionSpec as P

HEAD_DIM = 128
SEQ = ("seq_0", "seq_1")
DOC_SEQ = ("doc", "seq_0", "seq_1")


EPSILON = 1e-05
NEG_BIG = -1e30
HIGHEST = lax.Precision.HIGHEST


def neutral_like(x, identity):
    return jax.tree.map(
        lambda a, e: jnp.broadcast_to(jnp.asarray(e, a.dtype), a.shape), x, identity
    )


def carried_in(x, axes, combine, identity):
    before = start = neutral_like(x, identity)
    so_far = x
    for axis in reversed(axes):
        size, here = (lax.axis_size(axis), lax.axis_index(axis))
        pieces = jax.tree.map(lambda part: lax.all_gather(part, axis), so_far)
        inside, so_far = (start, start)
        for k in range(size):
            passed = k < here
            so_far = combine(so_far, jax.tree.map(lambda part: part[k], pieces))
            inside = jax.tree.map(lambda new, old: jnp.where(passed, new, old), so_far, inside)
        before = combine(inside, before)
    return before


def from_everyone(x, axis):
    copies = jnp.broadcast_to(x, (lax.axis_size(axis), *x.shape))
    return lax.all_to_all(copies, axis, split_axis=0, concat_axis=0, tiled=True)


def of_everyone(x, axis):
    everything = from_everyone(x, axis)
    return jnp.sum(everything, axis=0)


def in_one_piece(arrays, axis, dim, along):
    both = jnp.concatenate(arrays, axis=along)
    whole, at, done = (lax.all_gather(both, axis, axis=dim, tiled=True), 0, [])
    for a in arrays:
        done.append(lax.slice_in_dim(whole, at, at + a.shape[along], axis=along))
        at += a.shape[along]
    return tuple(done)


def chain_link(earlier, later):
    return (earlier[0] * later[0], later[0][:, None, None] * earlier[1] + later[1])


def body(
    length,
    residual,
    ssm_input,
    state_in,
    state_out,
    step_raw,
    decay_rate,
    ssm_gain,
    out_weight,
    norm_gain,
    query_weight,
    key_weight,
    value_weight,
):
    rows = residual.shape[0]
    local_heads = decay_rate.shape[0]
    head_width = ssm_input.shape[1] // local_heads
    seq_index = lax.axis_index(SEQ)
    limit = length[0]
    positions = seq_index * rows + jnp.arange(rows, dtype=jnp.int32)
    live_rows = positions < limit
    live = live_rows.astype(jnp.float32)
    delta = live[None, :] * jax.nn.softplus(step_raw)
    cumlog = jnp.cumsum(-decay_rate[:, None] * delta, axis=1)
    inputs = ssm_input.astype(jnp.float32).reshape(rows, local_heads, head_width)
    inner = jnp.dot(state_out, state_in.T, preferred_element_type=jnp.float32)
    causal = jnp.arange(rows)[:, None] >= jnp.arange(rows)[None, :]
    spread = cumlog[:, :, None] - cumlog[:, None, :]
    mixing = (
        jnp.where(causal[None], jnp.exp(jnp.where(causal[None], spread, 0.0)), 0.0)
        * inner[None]
        * delta[:, None, :]
    )
    within = jnp.einsum("hts,shp->thp", mixing, inputs, precision=HIGHEST)
    tail = jnp.exp(cumlog[:, -1:] - cumlog) * delta
    local_state = jnp.einsum(
        "hs,shp,sn->hpn", tail, inputs, state_in.astype(jnp.float32), precision=HIGHEST
    )
    block_decay = jnp.exp(cumlog[:, -1])
    prefix = carried_in(
        (block_decay, local_state),
        SEQ,
        chain_link,
        (jnp.ones_like(block_decay), jnp.zeros_like(local_state)),
    )
    incoming = prefix[1]
    carried = jnp.einsum("hpn,tn->thp", incoming, state_out.astype(jnp.float32), precision=HIGHEST)
    ssm_out = (within + jnp.exp(cumlog).T[:, :, None] * carried) * live[:, None, None]
    mean_square = jnp.mean(ssm_out * ssm_out, axis=2, keepdims=True)
    normed = (
        ssm_out * lax.rsqrt(mean_square + EPSILON) * ssm_gain.reshape(local_heads, head_width)
    ).astype(jnp.bfloat16)
    normed = normed.reshape(rows, local_heads * head_width)
    partial_value = jnp.dot(normed, out_weight, preferred_element_type=jnp.float32)
    model_width = norm_gain.shape[0]
    own_width = residual.shape[1]
    projected = lax.psum_scatter(partial_value, "head", scatter_dimension=1, tiled=True)
    layer_out = (residual.astype(jnp.float32) + projected).astype(jnp.bfloat16)
    widened = layer_out.astype(jnp.float32)
    squares = of_everyone(jnp.sum(widened * widened, axis=1), "head")
    piece_gain = lax.dynamic_slice_in_dim(norm_gain, lax.axis_index("head") * own_width, own_width)
    scaled = (widened * lax.rsqrt(squares / model_width + EPSILON)[:, None] * piece_gain).astype(
        jnp.bfloat16
    )
    attn_in = lax.all_gather(scaled, "head", axis=1, tiled=True)
    queries = jnp.dot(attn_in, query_weight, preferred_element_type=jnp.float32).astype(
        jnp.bfloat16
    )
    keys = jnp.dot(attn_in, key_weight, preferred_element_type=jnp.float32).astype(jnp.bfloat16)
    values = jnp.dot(attn_in, value_weight, preferred_element_type=jnp.float32).astype(jnp.bfloat16)
    query_local = query_weight.shape[1] // HEAD_DIM
    kv_local = key_weight.shape[1] // HEAD_DIM
    group_size = query_local // kv_local
    grouped = queries.reshape(rows, kv_local, group_size, HEAD_DIM)
    best = jnp.full((rows, query_local), NEG_BIG, jnp.float32)
    key_piece, value_piece = in_one_piece((keys, values), SEQ, 0, 1)
    count = key_piece.shape[0]
    key_pos = jnp.arange(count, dtype=jnp.int32)
    allowed = (key_pos[None, :] <= positions[:, None]) & (key_pos[None, :] < limit)
    scores = jnp.einsum(
        "tkgd,rkd->tkgr",
        grouped,
        key_piece.reshape(count, kv_local, HEAD_DIM),
        preferred_element_type=jnp.float32,
    ) * HEAD_DIM ** (-0.5)
    scores = scores.reshape(rows, query_local, count)
    allowed_wide = allowed[:, None, :]
    masked = jnp.where(allowed_wide, scores, NEG_BIG)
    new_best = jnp.maximum(best, jnp.max(masked, axis=2))
    weights = jnp.where(allowed_wide, jnp.exp(masked - new_best[:, :, None]), 0.0)
    total = jnp.sum(weights, axis=2)
    update = jnp.einsum(
        "tkgr,rkd->tkgd",
        weights.astype(jnp.bfloat16).reshape(rows, kv_local, group_size, count),
        value_piece.reshape(count, kv_local, HEAD_DIM),
        preferred_element_type=jnp.float32,
    )
    accum = update.reshape(rows, query_local, HEAD_DIM)
    folded = (new_best, total, accum)
    total = folded[1]
    accum = folded[2]
    safe_total = jnp.where(live_rows[:, None], total, 1.0)
    head_out = (
        (accum / safe_total[:, :, None] * live[:, None, None])
        .astype(jnp.bfloat16)
        .reshape(rows, query_local * HEAD_DIM)
    )
    return (layer_out, head_out)


def solution(mesh):
    torus = Mesh(
        mesh.devices.reshape(mesh.shape["doc"], 8, 2, mesh.shape["head"]),
        ("doc", "seq_0", "seq_1", "head"),
    )
    in_specs = (
        P("doc"),
        P(DOC_SEQ, "head"),
        P(DOC_SEQ, "head"),
        P(DOC_SEQ, None),
        P(DOC_SEQ, None),
        P(("doc", "head"), SEQ),
        P("head"),
        P("head"),
        P("head", None),
        P(),
        P(None, "head"),
        P(None, "head"),
        P(None, "head"),
    )
    out_specs = (P(DOC_SEQ, "head"), P(DOC_SEQ, "head"))
    return jax.shard_map(body, mesh=torus, in_specs=in_specs, out_specs=out_specs, check_vma=False)
```

profile of v0, /device:TPU:513, one launch (start us, length us, event | category | flops | bytes accessed | tf_op | source)
XLA Modules:
  0.0 267.5 jit_solution(8463071654418633136)
XLA Ops:
  8.0 1.3 dynamic-slice.1
  9.3 1.3 dynamic-slice
  14.5 22.5 %all-reduce = f32[16]{0:T(128)S(1)} all-reduce(f32[16]{0:T(128)S(1)} %dynamic-update-slice), channel_id=2, replica_groups=mesh['doc'=2,'seq_0'=8,'seq_1'=2,'head'=8] {'seq_1'}, use_global_device_ids=true, to_apply=%add | all-reduce | flops 16 | bytes 128
  37.1 1.1 copy.38
  38.3 1.2 fusion.36
  39.5 2.2 all-gather.1
  43.6 10.8 %all-reduce.1 = f32[64]{0:T(128)S(1)} all-reduce(f32[64]{0:T(128)S(1)} %get-tuple-element.14), channel_id=4, replica_groups=mesh['doc'=2,'seq_0'=8,'seq_1'=2,'head'=8] {'seq_0'}, use_global_device_ids=true, to_apply=%add.1 | all-reduce | flops 64 | bytes 512
  55.6 1.8 fusion.17
  57.4 22.4 %all-gather.7.cloned.1.call-done = f32[8,8,64,128]{3,2,1,0:T(8,128)} async-done(((f32[1,8,64,128]{3,2,1,0:T(8,128)}), f32[8,8,64,128]{3,2,1,0:T(8,128)}) %all-gather.7.cloned.1.call-update) | async-done | bytes 2097168 | tf_op jit(solution)/shard_map/all_gather | solution.py:28
  79.8 2.3 multiply_reduce_fusion
  82.6 3.2 %fusion.118 = f32[256,4096]{1,0:T(8,128)} fusion(bf16[256,512]{0,1:T(8,128)(2,1)S(1)} %bitcast.182, bf16[512,4096]{1,0:T(8,128)(2,1)S(1)} %copy-done.1), kind=kOutput, calls=%fused_computation.154 | convolution fusion | flops 1073741824 | bytes 8650752 | tf_op jit(solution)/shard_map/dot_general | solution.py:115
  85.9 59.2 %reduce-scatter.2.cloned.1.call-done = f32[256,512]{1,0:T(8,128)} async-done(((f32[256,4096]{1,0:T(8,128)}), f32[256,512]{1,0:T(8,128)}) %reduce-scatter.2.cloned.1.call-update) | async-done | bytes 524304 | tf_op jit(solution)/shard_map/reduce_scatter | solution.py:118
  145.0 1.2 fusion.31
  146.9 4.2 %all-to-all-start = ((f32[8,1,256]{2,1,0:T(1,128)}), f32[8,1,256]{2,1,0:T(1,128)S(1)}, u32[]{:S(2)}, u32[]{:S(2)}) async-start(f32[8,1,256]{2,1,0:T(1,128)} %broadcast_in_dim.96), calls=%async_computation.1 | async-start | bytes 16384 | tf_op jit(solution)/shard_map/all_to_all | solution.py:40
  152.0 5.7 %all-to-all-done = f32[8,1,256]{2,1,0:T(1,128)S(1)} async-done(((f32[8,1,256]{2,1,0:T(1,128)}), f32[8,1,256]{2,1,0:T(1,128)S(1)}, u32[]{:S(2)}, u32[]{:S(2)}) %all-to-all-start) | async-done | bytes 8224 | tf_op jit(solution)/shard_map/all_to_all | solution.py:40
  158.9 35.7 %all-gather.9.cloned.1.call-done = bf16[256,4096]{1,0:T(8,128)(2,1)} async-done(((bf16[256,512]{1,0:T(8,128)(2,1)}), bf16[256,4096]{1,0:T(8,128)(2,1)}) %all-gather.9.cloned.1.call-update) | async-done | bytes 2097168 | tf_op jit(solution)/shard_map/all_gather | solution.py:126
  194.7 2.6 convolution_convert_fusion.1
  197.2 2.7 %convolution_convert_fusion.2 = bf16[256,128]{0,1:T(8,128)(2,1)S(1)} fusion(bf16[256,4096]{1,0:T(8,128)(2,1)} %all-gather.9.cloned.1.call-done, bf16[4096,128]{1,0:T(8,128)(2,1)} %param.24), kind=kOutput, calls=%fused_computation.28 | convolution fusion | flops 268468224 | bytes 3211264 | tf_op jit(solution)/shard_map/dot_general | solution.py:130
  200.7 2.9 %fusion.9 = pred[256,4096]{0,1:T(8,128)(4,1)} fusion(s32[256]{0:T(256)S(1)} %iota_add_fusion, pred[4096]{0:T(1024)(128)(4,1)S(1)} %iota_compare_fusion.2), kind=kLoop, calls=%fused_computation.12 | loop fusion | flops 2097152 | bytes 1053696 | tf_op jit(solution)/shard_map/and | solution.py:140
  203.6 4.1 %fusion.23 = bf16[32,4,8,128]{3,2,1,0:T(8,128)(2,1)} fusion(bf16[256,4096]{1,0:T(8,128)(2,1)S(1)} %copy-done.2, bf16[4096,512]{1,0:T(8,128)(2,1)} %param.23), kind=kOutput, calls=%fused_computation.26 | convolution fusion | flops 1073872896 | bytes 6553600 | tf_op jit(solution)/shard_map/dot_general | solution.py:127
  207.7 38.6 %all-gather.11.cloned.1.call-done = bf16[4096,256]{0,1:T(8,128)(2,1)} async-done(((bf16[256,256]{0,1:T(8,128)(2,1)}), bf16[4096,256]{0,1:T(8,128)(2,1)}) %all-gather.11.cloned.1.call-update) | async-done | bytes 2097168 | tf_op jit(solution)/shard_map/all_gather | solution.py:50
  246.3 4.3 %fusion.4 = (f32[256,4]{0,1:T(4,128)S(1)}, f32[4096,256,4]{1,0,2:T(8,128)S(1)}) fusion(pred[256,4096]{0,1:T(8,128)(4,1)} %fusion.9, bf16[32,4,8,128]{3,2,1,0:T(8,128)(2,1)} %fusion.23, bf16[4096,256]{0,1:T(8,128)(2,1)} %all-gather.11.cloned.1.call-done), kind=kOutput, calls=%fused_computation.7 | convolution fusion | flops 1086323712 | bytes 19140608 | tf_op jit(solution)/shard_map/tkgd,rkd->tkgr/dot_general | solution.py:141
  250.7 4.2 %select_reduce_fusion = f32[256,4]{0,1:T(4,128)S(1)} fusion(f32[4096,256,4]{1,0,2:T(8,128)S(1)} %get-tuple-element.27, f32[256,4]{0,1:T(4,128)S(1)} %broadcast_maximum_fusion, pred[256,4096]{0,1:T(8,128)(4,1)S(1)} %copy-done.3), kind=kLoop, calls=%fused_computation.6 | loop fusion | flops 20970496 | bytes 17833984 | tf_op jit(solution)/shard_map/reduce_sum | solution.py:152
  254.9 4.6 %fusion.6 = f32[128,256,4]{1,0,2:T(8,128)S(1)} fusion(f32[4096,256,4]{1,0,2:T(8,128)S(1)} %get-tuple-element.27, f32[256,4]{0,1:T(4,128)S(1)} %broadcast_maximum_fusion, pred[256,4096]{0,1:T(8,128)(4,1)S(1)} %copy-done.3, bf16[4096,256]{0,1:T(8,128)(2,1)S(1)} %copy-done.7), kind=kOutput, calls=%fused_computation.9 | convolution fusion | flops 1094713344 | bytes 19402752 | tf_op jit(solution)/shard_map/tkgr,rkd->tkgd/dot_general | solution.py:153
  (59 shorter events, 11.2 us)
Async XLA Ops:
  7.2 187.5 %copy-start = (bf16[4096,128]{1,0:T(8,128)(2,1)S(1)}, bf16[4096,128]{1,0:T(8,128)(2,1)}, u32[]{:S(2)}) copy-start(bf16[4096,128]{1,0:T(8,128)(2,1)} %param.25) | copy-start | bytes 3145732
  7.2 72.6 %all-gather.7.cloned.1.call-start = ((), (), s32[]{:S(2)}) async-start(), calls=%async_computation.2 | async-start | bytes 2359296 | tf_op jit(solution)/shard_map/all_gather | solution.py:28
  37.1 42.7 %copy-start.6 = (bf16[256,128]{1,0:T(8,128)(2,1)S(1)}, bf16[256,128]{1,0:T(8,128)(2,1)}, u32[]{:S(2)}) copy-start(bf16[256,128]{1,0:T(8,128)(2,1)} %param.17) | copy-start | bytes 196612
  42.8 102.3 %reduce-scatter.2.cloned.1.call-start = ((), (), s32[]{:S(2)}) async-start(), calls=%async_computation.3 | async-start | bytes 4718592 | tf_op jit(solution)/shard_map/reduce_scatter | solution.py:118
  79.8 2.8 %copy-start.1 = (bf16[512,4096]{1,0:T(8,128)(2,1)S(1)}, bf16[512,4096]{1,0:T(8,128)(2,1)}, u32[]{:S(2)}) copy-start(bf16[512,4096]{1,0:T(8,128)(2,1)} %param.21) | copy-start | bytes 12582916
  85.8 59.2 %copy-start.5 = (bf16[256,512]{1,0:T(8,128)(2,1)S(1)}, bf16[256,512]{1,0:T(8,128)(2,1)}, u32[]{:S(2)}) copy-start(bf16[256,512]{1,0:T(8,128)(2,1)} %param.14) | copy-start | bytes 786436
  146.2 57.3 %copy-start.4 = (bf16[256,512]{1,0:T(8,128)(2,1)}, bf16[256,512]{1,0:T(8,128)(2,1)S(1)}, u32[]{:S(2)}) copy-start(bf16[256,512]{1,0:T(8,128)(2,1)S(1)} %get-tuple-element.5) | copy-start | bytes 786436
  146.9 10.8 %all-to-all-start = ((f32[8,1,256]{2,1,0:T(1,128)}), f32[8,1,256]{2,1,0:T(1,128)S(1)}, u32[]{:S(2)}, u32[]{:S(2)}) async-start(f32[8,1,256]{2,1,0:T(1,128)} %broadcast_in_dim.96), calls=%async_computation.1 | async-start | bytes 16384 | tf_op jit(solution)/shard_map/all_to_all | solution.py:40
  151.1 43.5 %all-gather.9.cloned.1.call-start = ((), (), s32[]{:S(2)}) async-start(), calls=%async_computation.4 | async-start | bytes 2359296 | tf_op jit(solution)/shard_map/all_gather | solution.py:126
  158.7 87.6 %all-gather.11.cloned.1.call-start = ((), (), s32[]{:S(2)}) async-start(), calls=%async_computation.5 | async-start | bytes 2228224 | tf_op jit(solution)/shard_map/all_gather | solution.py:50
  194.7 8.9 %copy-start.2 = (bf16[256,4096]{1,0:T(8,128)(2,1)S(1)}, bf16[256,4096]{1,0:T(8,128)(2,1)}, u32[]{:S(2)}) copy-start(bf16[256,4096]{1,0:T(8,128)(2,1)} %all-gather.9.cloned.1.call-done) | copy-start | bytes 6291460
  207.7 42.9 %copy-start.3 = (pred[256,4096]{0,1:T(8,128)(4,1)S(1)}, pred[256,4096]{0,1:T(8,128)(4,1)}, u32[]{:S(2)}) copy-start(pred[256,4096]{0,1:T(8,128)(4,1)} %fusion.9) | copy-start | bytes 3145732
  250.7 4.2 %copy-start.7 = (bf16[4096,256]{0,1:T(8,128)(2,1)S(1)}, bf16[4096,256]{0,1:T(8,128)(2,1)}, u32[]{:S(2)}) copy-start(bf16[4096,256]{0,1:T(8,128)(2,1)} %all-gather.11.cloned.1.call-done) | copy-start | bytes 6291460
Sparse Core Ops, SparseCore 0:
  42.9 36.8 all-gather.6
  86.0 58.9 reduce-scatter.1
  158.8 35.8 all-gather.8
  200.7 45.5 all-gather.10
where the time goes:
time: 268 us; the launch traced here: 267 us
  waiting for transfers between devices  162 us (60%)
  blocking collectives  35.6 us (13%)
  matrix products  27.9 us (10%)
  between operations  16 us (6%)
  other arithmetic  14 us (5%)
  local copies, waits for them, and re-layouts  7.41 us (3%)
  starting transfers between devices  4.67 us (2%)
    reduce_scatter x1, waiting for transfers between devices, body(): lax.psum_scatter(partial_value, 'head', scatter_dimension=1, tiled=True)  59.2 us
    all_gather x1, waiting for transfers between devices, in_one_piece(): whole, at, done = (lax.all_gather(both, axis, axis=dim, tiled=True), 0, [])  38.6 us
    all_gather x1, waiting for transfers between devices, body(): attn_in = lax.all_gather(scaled, 'head', axis=1, tiled=True)  35.7 us
    unnamed x2, blocking collectives  33.3 us
    all_gather x1, waiting for transfers between devices, carried_in(): pieces = jax.tree.map(lambda part: lax.all_gather(part, axis), so_far)  22.4 us
    all_to_all x1, waiting for transfers between devices, from_everyone(): return lax.all_to_all(copies, axis, split_axis=0, concat_axis=0, tiled=True)  5.74 us
  transfers between devices with their start and end apart: 5, of which 5 were waited for; matrix products, arithmetic and copies ran while one was open for 4% of the time, Pallas kernels for 0%

commit v1 on v0

v1 whole, which is shorter than its diff:
```python
import functools

import jax
import jax.numpy as jnp
from jax import lax
from jax.experimental import pallas as pl
from jax.experimental.pallas import tpu as pltpu
from jax.sharding import Mesh
from jax.sharding import PartitionSpec as P

HEAD_DIM = 128
EPSILON = 1e-05
DOC_SEQ = ("doc", "seq_0", "seq_1")
SEQ = ("seq_0", "seq_1")
MESH = pl.DeviceIdType.MESH
VMEM = pl.BlockSpec(memory_space=pltpu.VMEM)
SMEM = pl.BlockSpec(memory_space=pltpu.SMEM)
F32 = jnp.float32
BF16 = jnp.bfloat16

SUB = 4


def contract(a, b, dims):
    return lax.dot_general(a, b, (dims, ((), ())), preferred_element_type=F32)


def two_terms(x):
    high = x.astype(BF16)
    return high, (x - high.astype(F32)).astype(BF16)


def seq_peer(index):
    return {"seq_0": index // 2, "seq_1": index % 2}


def ssm_kernel(
    n,
    length_ref,
    x_ref,
    b_ref,
    c_ref,
    step_ref,
    decay_ref,
    gain_ref,
    normed_ref,
    stage,
    arrived,
    prefix,
    incoming,
    within,
    out_sems,
    in_sems,
    back_sems,
    home_sems,
):
    me = lax.axis_index("seq_0") * 2 + lax.axis_index("seq_1")
    rows, width = x_ref.shape
    heads = step_ref.shape[0]
    head_width = width // heads
    piece = width // n
    per_head = head_width // piece

    barrier = pltpu.get_barrier_semaphore()
    for o in range(1, n):
        pl.semaphore_signal(
            barrier, inc=1, device_id=seq_peer(lax.rem(me + o, n)), device_id_type=MESH
        )

    limit = length_ref[0]
    along = lax.broadcasted_iota(jnp.int32, (1, rows), 1) + me * rows
    live_row = (along < limit).astype(F32)
    down = lax.broadcasted_iota(jnp.int32, (rows, 1), 0) + me * rows
    live_col = (down < limit).astype(F32)
    raw = step_ref[...]
    delta = live_row * (jnp.maximum(raw, 0.0) + jnp.log1p(jnp.exp(-jnp.abs(raw))))
    t_of = lax.broadcasted_iota(jnp.int32, (rows, rows), 0)
    s_of = lax.broadcasted_iota(jnp.int32, (rows, rows), 1)
    causal = t_of >= s_of
    upper = (t_of <= s_of).astype(F32)
    cumlog = lax.dot_general(
        -decay_ref[...] * delta,
        upper,
        (((1,), (0,)), ((), ())),
        precision=lax.Precision.HIGHEST,
        preferred_element_type=F32,
    )
    last = cumlog[:, rows - 1 : rows]
    tail_t = jnp.transpose(jnp.exp(last - cumlog) * delta)
    cumlog_t = jnp.transpose(cumlog)
    block_decay = jnp.broadcast_to(jnp.exp(last), (heads, 128))
    lanes = lax.broadcasted_iota(jnp.int32, (rows, 128), 1)
    first = lanes < head_width

    for pair in range(width // 128):
        a, b = 2 * pair, 2 * pair + 1
        scale = jnp.where(first, tail_t[:, a : a + 1], tail_t[:, b : b + 1])
        high, low = two_terms(x_ref[:, 128 * pair : 128 * (pair + 1)].astype(F32) * scale)
        state = contract(high, b_ref[...], ((0,), (0,))) + contract(low, b_ref[...], ((0,), (0,)))
        for q in range(128 // piece):
            j = pair * (128 // piece) + q
            stage[j, 0:piece] = state[q * piece : (q + 1) * piece]
            h = j // per_head
            stage[j, piece : piece + 8] = jnp.broadcast_to(block_decay[h : h + 1], (8, 128))

    pl.semaphore_wait(barrier, n - 1)

    def out_copy(o):
        peer = lax.rem(me + o, n)
        return pltpu.make_async_remote_copy(
            src_ref=stage.at[peer],
            dst_ref=arrived.at[me],
            send_sem=out_sems.at[o],
            recv_sem=in_sems.at[o],
            device_id=seq_peer(peer),
            device_id_type=MESH,
        )

    order = sorted(range(1, n), key=lambda o: -min(o, n - o))
    for o in order:
        out_copy(o).start()
    arrived[me] = stage[me]

    inner = contract(c_ref[...], b_ref[...], ((1,), (1,)))
    for pair in range(width // 128):
        values = x_ref[:, 128 * pair : 128 * (pair + 1)]
        parts = []
        for h in (2 * pair, 2 * pair + 1):
            spread = cumlog_t[:, h : h + 1] - cumlog[h : h + 1, :]
            mixing = jnp.exp(jnp.where(causal, spread, -1e30)) * inner * delta[h : h + 1, :]
            high, low = two_terms(mixing)
            parts.append(
                contract(high, values, ((1,), (0,))) + contract(low, values, ((1,), (0,)))
            )
        within[:, 128 * pair : 128 * (pair + 1)] = jnp.where(first, parts[0], parts[1])

    for o in order:
        out_copy(o).wait_recv()
    carry = jnp.zeros((piece, 128), F32)
    for i in range(n):
        prefix[i] = carry
        carry = arrived[i, piece : piece + 1] * carry + arrived[i, 0:piece]

    def home_copy(o):
        peer = lax.rem(me + o, n)
        return pltpu.make_async_remote_copy(
            src_ref=prefix.at[peer],
            dst_ref=incoming.at[me],
            send_sem=back_sems.at[o],
            recv_sem=home_sems.at[o],
            device_id=seq_peer(peer),
            device_id_type=MESH,
        )

    for o in order:
        home_copy(o).start()
    incoming[me] = prefix[me]
    for o in order:
        home_copy(o).wait_recv()

    group = (
        lax.broadcasted_iota(jnp.int32, (128, 128), 0) // head_width
        == lax.broadcasted_iota(jnp.int32, (128, 128), 1) // head_width
    ).astype(BF16)
    grown = jnp.exp(cumlog_t)
    for pair in range(width // 128):
        a, b = 2 * pair, 2 * pair + 1
        count = 128 // piece
        state = incoming[pair * count : (pair + 1) * count].reshape(128, 128)
        high, low = two_terms(state)
        carried = contract(c_ref[...], high, ((1,), (1,))) + contract(
            c_ref[...], low, ((1,), (1,))
        )
        scale = jnp.where(first, grown[:, a : a + 1], grown[:, b : b + 1])
        y = (within[:, 128 * pair : 128 * (pair + 1)] + scale * carried) * live_col
        high, low = two_terms(y * y)
        mean = (contract(high, group, ((1,), (0,))) + contract(low, group, ((1,), (0,)))) * (
            1.0 / head_width
        )
        cols = slice(128 * pair, 128 * (pair + 1))
        normed_ref[:, cols] = (y * lax.rsqrt(mean + EPSILON) * gain_ref[:, cols]).astype(BF16)

    for o in order:
        out_copy(o).wait_send()
        home_copy(o).wait_send()


def ssm_layer(length, ssm_input, state_in, state_out, step_raw, decay_rate, ssm_gain):
    rows, width = ssm_input.shape
    n = lax.axis_size(SEQ)
    piece = width // n
    return pl.pallas_call(
        functools.partial(ssm_kernel, n),
        out_shape=jax.ShapeDtypeStruct((rows, width), BF16),
        in_specs=[SMEM] + [VMEM] * 6,
        out_specs=VMEM,
        scratch_shapes=[
            pltpu.VMEM((n, piece + 8, 128), F32),
            pltpu.VMEM((n, piece + 8, 128), F32),
            pltpu.VMEM((n, piece, 128), F32),
            pltpu.VMEM((n, piece, 128), F32),
            pltpu.VMEM((rows, width), F32),
            pltpu.SemaphoreType.DMA((n,)),
            pltpu.SemaphoreType.DMA((n,)),
            pltpu.SemaphoreType.DMA((n,)),
            pltpu.SemaphoreType.DMA((n,)),
        ],
        compiler_params=pltpu.CompilerParams(collective_id=0, has_side_effects=True),
        name="ssm_layer",
    )(
        length,
        ssm_input,
        state_in,
        state_out,
        step_raw,
        decay_rate.reshape(-1, 1),
        ssm_gain.reshape(1, -1),
    )


def depth(direction, s, n):
    long_way = (s < SUB // 2) == (direction == 0)
    return n // 2 if long_way else n - 1 - n // 2


def project_kernel(
    n,
    normed_ref,
    weight_ref,
    residual_ref,
    layer_ref,
    full_ref,
    outgoing,
    arrived,
    sum_send,
    sum_recv,
    all_send,
    all_recv,
):
    me = lax.axis_index("head")
    rows = normed_ref.shape[0]
    width = residual_ref.shape[1]
    block = rows // SUB
    half = rows // 2
    neighbour = (lax.rem(me + n - 1, n), lax.rem(me + 1, n))

    barrier = pltpu.get_barrier_semaphore()
    for d in (0, 1):
        pl.semaphore_signal(
            barrier, inc=1, device_id={"head": neighbour[d]}, device_id_type=MESH
        )
    pl.semaphore_wait(barrier, 2)

    def away(d, steps):
        return lax.rem(me + (n - steps if d == 0 else steps), n)

    def partial(j, side):
        cols = pl.ds(pl.multiple_of(j * width, width), width)
        return contract(
            normed_ref[side * half : (side + 1) * half], weight_ref[:, cols], ((1,), (0,))
        )

    def sum_copy(d, level, s):
        return pltpu.make_async_remote_copy(
            src_ref=outgoing.at[d, level, s],
            dst_ref=arrived.at[d, level, s],
            send_sem=sum_send.at[d, level, s],
            recv_sem=sum_recv.at[d, level, s],
            device_id={"head": neighbour[d]},
            device_id_type=MESH,
        )

    def all_copy(d, level, s):
        owner = away(1 - d, level)
        at = (owner, pl.ds(s * block, block))
        return pltpu.make_async_remote_copy(
            src_ref=full_ref.at[at],
            dst_ref=full_ref.at[at],
            send_sem=all_send.at[d, level, s],
            recv_sem=all_recv.at[d, level, s],
            device_id={"head": neighbour[d]},
            device_id_type=MESH,
        )

    most = n // 2
    for level in range(most):
        for side in (0, 1):
            for d in (0, 1):
                hops = depth(d, side * (SUB // 2), n)
                if level >= hops:
                    continue
                product = partial(away(d, hops - level), side)
                for k in range(SUB // 2):
                    s = side * (SUB // 2) + k
                    value = product[k * block : (k + 1) * block]
                    if level > 0:
                        sum_copy(d, level - 1, s).wait_recv()
                        value = value + arrived[d, level - 1, s].astype(F32)
                    outgoing[d, level, s] = value.astype(BF16)
                    sum_copy(d, level, s).start()

    for side in (0, 1):
        product = partial(me, side)
        for k in range(SUB // 2):
            s = side * (SUB // 2) + k
            here = slice(s * block, (s + 1) * block)
            value = residual_ref[here].astype(F32) + product[k * block : (k + 1) * block]
            for d in (0, 1):
                last = depth(d, s, n) - 1
                sum_copy(d, last, s).wait_recv()
                value = value + arrived[d, last, s].astype(F32)
            value = value.astype(BF16)
            layer_ref[here] = value
            full_ref[me, here] = value
            for d in (0, 1):
                all_copy(d, 0, s).start()

    for level in range(1, most):
        for s in range(SUB):
            for d in (0, 1):
                if level < depth(d, s, n):
                    all_copy(d, level - 1, s).wait_recv()
                    all_copy(d, level, s).start()
    for s in range(SUB):
        for d in (0, 1):
            all_copy(d, depth(d, s, n) - 1, s).wait_recv()
    for s in range(SUB):
        for d in (0, 1):
            for level in range(depth(d, s, n)):
                sum_copy(d, level, s).wait_send()
                all_copy(d, level, s).wait_send()


def project(normed, out_weight, residual):
    rows, width = residual.shape
    n = lax.axis_size("head")
    slots = (2, n // 2, SUB)
    return pl.pallas_call(
        functools.partial(project_kernel, n),
        out_shape=(
            jax.ShapeDtypeStruct((rows, width), BF16),
            jax.ShapeDtypeStruct((n, rows, width), BF16),
        ),
        in_specs=[VMEM] * 3,
        out_specs=(VMEM, VMEM),
        scratch_shapes=[
            pltpu.VMEM((*slots, rows // SUB, width), BF16),
            pltpu.VMEM((*slots, rows // SUB, width), BF16),
            pltpu.SemaphoreType.DMA(slots),
            pltpu.SemaphoreType.DMA(slots),
            pltpu.SemaphoreType.DMA(slots),
            pltpu.SemaphoreType.DMA(slots),
        ],
        compiler_params=pltpu.CompilerParams(
            collective_id=1, has_side_effects=True, vmem_limit_bytes=40 << 20
        ),
        name="project",
    )(normed, out_weight, residual)


def attend_kernel(
    n,
    length_ref,
    full_ref,
    gain_ref,
    wq_ref,
    wk_ref,
    wv_ref,
    out_ref,
    attn_in,
    queries,
    kv,
    best,
    total,
    accum,
    ring_send,
    ring_recv,
    twin_send,
    twin_recv,
):
    y = lax.axis_index("seq_0")
    core = lax.axis_index("seq_1")
    me = y * 2 + core
    chunks, rows, width = full_ref.shape
    heads = width // HEAD_DIM
    neighbour = (lax.rem(y + n - 1, n), lax.rem(y + 1, n))

    barrier = pltpu.get_barrier_semaphore()
    for d in (0, 1):
        pl.semaphore_signal(
            barrier, inc=1, device_id={"seq_0": neighbour[d]}, device_id_type=MESH
        )
    pl.semaphore_signal(barrier, inc=1, device_id={"seq_1": 1 - core}, device_id_type=MESH)

    squares = jnp.zeros((rows, 1), F32)
    for j in range(chunks):
        wide = full_ref[j].astype(F32)
        squares = squares + jnp.sum(wide * wide, axis=1, keepdims=True)
    inverse = lax.rsqrt(squares * (1.0 / (chunks * width)) + EPSILON)
    keys = jnp.zeros((rows, HEAD_DIM), F32)
    values = jnp.zeros((rows, HEAD_DIM), F32)
    for j in range(chunks):
        wide = full_ref[j].astype(F32) * inverse * gain_ref[j : j + 1]
        scaled = wide.astype(BF16)
        attn_in[j] = scaled
        down = slice(j * width, (j + 1) * width)
        keys = keys + contract(scaled, wk_ref[down], ((1,), (0,)))
        values = values + contract(scaled, wv_ref[down], ((1,), (0,)))
    kv[0, me] = keys.astype(BF16)
    kv[1, me] = values.astype(BF16)

    def hops(d, kind):
        long_way = (kind == 0) == (d == 1)
        return n // 2 if long_way else n - 1 - n // 2

    def owner_chip(d, level):
        return lax.rem(y + (level if d == 0 else n - level), n)

    def ring_copy(d, level, kind):
        at = (kind, owner_chip(d, level) * 2 + core)
        return pltpu.make_async_remote_copy(
            src_ref=kv.at[at],
            dst_ref=kv.at[at],
            send_sem=ring_send.at[d, level, kind],
            recv_sem=ring_recv.at[d, level, kind],
            device_id={"seq_0": neighbour[d]},
            device_id_type=MESH,
        )

    def twin_copy(d, level, kind, mine=True):
        chip = y if level < 0 else owner_chip(d, level + 1)
        at = (kind, chip * 2 + (core if mine else 1 - core))
        return pltpu.make_async_remote_copy(
            src_ref=kv.at[at],
            dst_ref=kv.at[at],
            send_sem=twin_send.at[d, level + 1, kind],
            recv_sem=twin_recv.at[d, level + 1, kind],
            device_id={"seq_1": 1 - core},
            device_id_type=MESH,
        )

    pl.semaphore_wait(barrier, 3)
    for kind in (0, 1):
        for d in (1, 0):
            ring_copy(d, 0, kind).start()
    for kind in (0, 1):
        twin_copy(0, -1, kind).start()

    product = jnp.zeros((rows, width), F32)
    for j in range(chunks):
        down = slice(j * width, (j + 1) * width)
        product = product + contract(attn_in[j], wq_ref[down], ((1,), (0,)))
    queries[...] = product.astype(BF16)

    scale = HEAD_DIM**-0.5 * 1.4426950408889634
    t_of = lax.broadcasted_iota(jnp.int32, (rows, rows), 0)
    s_of = lax.broadcasted_iota(jnp.int32, (rows, rows), 1)
    causal = t_of >= s_of
    for h in range(heads):
        cols = slice(h * HEAD_DIM, (h + 1) * HEAD_DIM)
        scores = contract(queries[:, cols], kv[0, me], ((1,), (1,))) * scale
        scores = jnp.where(causal, scores, -1e30)
        top = jnp.max(scores, axis=1, keepdims=True)
        weights = jnp.exp2(scores - top)
        best[h] = jnp.broadcast_to(top, (rows, HEAD_DIM))
        total[h] = jnp.broadcast_to(jnp.sum(weights, axis=1, keepdims=True), (rows, HEAD_DIM))
        accum[h] = contract(weights.astype(BF16), kv[1, me], ((1,), (0,)))

    def fold(key_block, value_block):
        for h in range(heads):
            cols = slice(h * HEAD_DIM, (h + 1) * HEAD_DIM)
            scores = contract(queries[:, cols], key_block, ((1,), (1,))) * scale
            old = best[h][:, 0:1]
            top = jnp.maximum(old, jnp.max(scores, axis=1, keepdims=True))
            weights = jnp.exp2(scores - top)
            shrink = jnp.exp2(old - top)
            best[h] = jnp.broadcast_to(top, (rows, HEAD_DIM))
            total[h] = total[h] * shrink + jnp.sum(weights, axis=1, keepdims=True)
            accum[h] = accum[h] * shrink + contract(
                weights.astype(BF16), value_block, ((1,), (0,))
            )

    def chip_block(kind, chip):
        return kv[kind, pl.ds(chip * 2, 2)].reshape(2 * rows, HEAD_DIM)

    for kind in (0, 1):
        twin_copy(0, -1, kind, mine=False).wait_recv()

    @pl.when(core == 1)
    def _():
        fold(kv[0, y * 2], kv[1, y * 2])

    def forward(d, level):
        for kind in (0, 1):
            if level < hops(d, kind):
                ring_copy(d, level, kind).wait_recv()
                if level + 1 < hops(d, kind):
                    ring_copy(d, level + 1, kind).start()
                twin_copy(d, level, kind).start()

    def both(d, level):
        return all(level < hops(d, kind) for kind in (0, 1))

    for level in range(n // 2):
        for d in (1, 0):
            forward(d, level)
        for d in (1, 0):
            for kind in (0, 1):
                if level < hops(d, kind):
                    twin_copy(d, level, kind, mine=False).wait_recv()
        for d in (1, 0):
            if both(d, level) or (level < hops(1, 0) and d == 1):
                chip = owner_chip(d, level + 1)

                @pl.when(chip < y)
                def _():
                    fold(chip_block(0, chip), chip_block(1, chip))

    live = (
        lax.broadcasted_iota(jnp.int32, (rows, 1), 0) + me * rows < length_ref[0]
    ).astype(F32)
    for h in range(heads):
        cols = slice(h * HEAD_DIM, (h + 1) * HEAD_DIM)
        safe = jnp.where(live > 0.0, total[h], 1.0)
        out_ref[:, cols] = (accum[h] / safe * live).astype(BF16)

    for kind in (0, 1):
        twin_copy(0, -1, kind).wait_send()
        for d in (0, 1):
            for level in range(hops(d, kind)):
                ring_copy(d, level, kind).wait_send()
                twin_copy(d, level, kind).wait_send()


def attend(length, full, norm_gain, query_weight, key_weight, value_weight):
    chunks, rows, width = full.shape
    n = lax.axis_size("seq_0")
    heads = width // HEAD_DIM
    ring = (2, n // 2, 2)
    twin = (2, n // 2 + 1, 2)
    return pl.pallas_call(
        functools.partial(attend_kernel, n),
        out_shape=jax.ShapeDtypeStruct((rows, width), BF16),
        in_specs=[SMEM] + [VMEM] * 5,
        out_specs=VMEM,
        scratch_shapes=[
            pltpu.VMEM((chunks, rows, width), BF16),
            pltpu.VMEM((rows, width), BF16),
            pltpu.VMEM((2, 2 * n, rows, HEAD_DIM), BF16),
            pltpu.VMEM((heads, rows, HEAD_DIM), F32),
            pltpu.VMEM((heads, rows, HEAD_DIM), F32),
            pltpu.VMEM((heads, rows, HEAD_DIM), F32),
            pltpu.SemaphoreType.DMA(ring),
            pltpu.SemaphoreType.DMA(ring),
            pltpu.SemaphoreType.DMA(twin),
            pltpu.SemaphoreType.DMA(twin),
        ],
        compiler_params=pltpu.CompilerParams(
            collective_id=2, has_side_effects=True, vmem_limit_bytes=48 << 20
        ),
        name="attend",
    )(length, full, norm_gain.reshape(chunks, width), query_weight, key_weight, value_weight)


def body(
    length,
    residual,
    ssm_input,
    state_in,
    state_out,
    step_raw,
    decay_rate,
    ssm_gain,
    out_weight,
    norm_gain,
    query_weight,
    key_weight,
    value_weight,
):
    normed = ssm_layer(length, ssm_input, state_in, state_out, step_raw, decay_rate, ssm_gain)
    layer_out, full = project(normed, out_weight, residual)
    head_out = attend(length, full, norm_gain, query_weight, key_weight, value_weight)
    return layer_out, head_out


def solution(mesh):
    torus = Mesh(
        mesh.devices.reshape(mesh.shape["doc"], mesh.shape["seq"] // 2, 2, mesh.shape["head"]),
        ("doc", "seq_0", "seq_1", "head"),
    )
    in_specs = (
        P("doc"),
        P(DOC_SEQ, "head"),
        P(DOC_SEQ, "head"),
        P(DOC_SEQ, None),
        P(DOC_SEQ, None),
        P(("doc", "head"), SEQ),
        P("head"),
        P("head"),
        P("head", None),
        P(),
        P(None, "head"),
        P(None, "head"),
        P(None, "head"),
    )
    out_specs = (P(DOC_SEQ, "head"), P(DOC_SEQ, "head"))
    return jax.shard_map(body, mesh=torus, in_specs=in_specs, out_specs=out_specs, check_vma=False)
```

time: 268 us -> 122 us (0.46)
  waiting for transfers between devices: 162 us -> 0 us
  Pallas kernels: 0 us -> 113 us
  blocking collectives: 35.6 us -> 0 us
  matrix products: 27.9 us -> 0 us
  between operations: 16 us -> 1.37 us
  other arithmetic: 14 us -> 0 us
  starting transfers between devices: 4.67 us -> 0 us
    pallas_call x0 -> x3, Pallas kernels: none -> 113 us  [the longest x1 43.4 us: project(): pl.pallas_call(functools.partial(project_kernel, n), out_shape=(jax.Shape...]
    all_gather x3 -> x0, waiting for transfers between devices: 96.7 us -> none  [the longest x1 38.6 us: in_one_piece(): whole, at, done = (lax.all_gather(both, axis, axis=dim, tiled=True), 0, [])]
    reduce_scatter x1 -> x0, waiting for transfers between devices: 59.2 us -> none  [body(): lax.psum_scatter(partial_value, 'head', scatter_dimension=1, tiled=True)]
    unnamed x2 -> x0, blocking collectives: 33.3 us -> none
    dot_general x10 -> x0, matrix products: 27.9 us -> none  [the longest x1 4.55 us: body(): jnp.einsum('tkgr,rkd->tkgd', weights.astype(jnp.bfloat16).reshape(rows, k...]
    all_to_all x1 -> x0, waiting for transfers between devices: 5.74 us -> none  [from_everyone(): return lax.all_to_all(copies, axis, split_axis=0, concat_axis=0, tiled=True)]
    reduce_sum x3 -> x0, other arithmetic: 5.4 us -> none  [the longest x1 4.18 us: body(): total = jnp.sum(weights, axis=2)]
    all_to_all x1 -> x0, starting transfers between devices: 4.24 us -> none  [from_everyone(): return lax.all_to_all(copies, axis, split_axis=0, concat_axis=0, tiled=True)]
  transfers between devices with their start and end apart: 5 -> 0, of which waited for: 5 -> 0; matrix products, arithmetic and copies ran while one was open for 4% -> 0% of each run, Pallas kernels for 0% -> 0%
where the time goes in v1:
time: 122 us
  Pallas kernels  113 us (93%)
  local copies, waits for them, and re-layouts  8.04 us (7%)
  between operations  1.37 us (1%)
    pallas_call x1, Pallas kernels, project(): pl.pallas_call(functools.partial(project_kernel, n), out_shape=(jax.Shape...  43.4 us
    pallas_call x1, Pallas kernels, ssm_layer(): pl.pallas_call(functools.partial(ssm_kernel, n), out_shape=jax.ShapeDtype...  42 us
    pallas_call x1, Pallas kernels, attend(): pl.pallas_call(functools.partial(attend_kernel, n), out_shape=jax.ShapeDt...  27.3 us
    unnamed x14, local copies, waits for them, and re-layouts  6.72 us

profile of v1, /device:TPU:513, one launch (start us, length us, event | category | flops | bytes accessed | tf_op | source)
XLA Modules:
  0.0 122.1 jit_solution(7926984466411380307)
XLA Ops:
  0.6 0.0 copy-start.5
  1.3 1.3 %copy.15.decay_ref = f32[8,1]{1,0:T(8,128)} copy(f32[8,1]{0,1:T(1,128)} %bitcast.3) | data formatting | bytes 64 | tf_op jit(solution)/shard_map/reshape | solution.py:216
  2.6 42.0 %ssm_layer.1.normed_ref = bf16[256,512]{1,0:T(8,128)(2,1)} custom-call(s32[1]{0:T(128)S(6)} %copy.18.length_ref, bf16[256,512]{1,0:T(8,128)(2,1)} %x_ref.1, bf16[256,128]{1,0:T(8,128)(2,1)} %b_ref.1, bf16[256,128]{1,0:T(8,128)(2,1)} %c_ref.1, f32[8,256]{1,0:T(8,128)} %step_ref.1, f32[8,1]{1,0:T(8,128)} %copy.15.decay_ref, f32[1,512]{1,0:T(1,128)} %bitcast.2), custom_call_target="tpu_custom_call" | custom-call | tf_op jit(solution)/shard_map/ssm_layer/pallas_call | solution.py:192
  44.6 0.0 copy-start
  44.6 2.2 %copy-done = bf16[512,4096]{1,0:T(8,128)(2,1)S(1)} copy-done((bf16[512,4096]{1,0:T(8,128)(2,1)S(1)}, bf16[512,4096]{1,0:T(8,128)(2,1)}, u32[]{:S(2)}) %copy-start) | copy-done | bytes 4194328
  46.8 0.0 copy-start.3
  46.8 0.9 copy-done.3
  47.8 0.0 copy-start.4
  47.8 0.9 copy-done.4
  48.7 0.0 copy-start.1
  48.7 43.4 %project.1 = (bf16[256,512]{1,0:T(8,128)(2,1)S(1)}, bf16[8,256,512]{2,1,0:T(8,128)(2,1)S(1)}) custom-call(bf16[256,512]{1,0:T(8,128)(2,1)S(1)} %copy-done.3, bf16[512,4096]{1,0:T(8,128)(2,1)S(1)} %copy-done, bf16[256,512]{1,0:T(8,128)(2,1)S(1)} %copy-done.4), custom_call_target="tpu_custom_call" | custom-call | tf_op jit(solution)/shard_map/project/pallas_call | solution.py:338
  92.1 0.0 copy-done.5
  92.1 0.0 copy-done.1
  92.1 0.0 copy-start.2
  92.2 1.2 copy-done.2
  93.4 27.3 %attend.1 = bf16[256,512]{1,0:T(8,128)(2,1)S(1)} custom-call(s32[1]{0:T(128)S(6)} %copy.18.length_ref, bf16[8,256,512]{2,1,0:T(8,128)(2,1)S(1)} %get-tuple-element.5.full_ref, f32[8,512]{1,0:T(8,128)S(1)} %reshape.15.gain_ref, bf16[4096,512]{1,0:T(8,128)(2,1)} %wq_ref.1, bf16[4096,128]{1,0:T(8,128)(2,1)S(1)} %copy-done.1, bf16[4096,128]{1,0:T(8,128)(2,1)S(1)} %copy-done.2), custom_call_target="tpu_custom_call" | custom-call | tf_op jit(solution)/shard_map/attend/pallas_call | solution.py:541
  120.7 0.7 copy.19
  121.4 0.7 copy.20
  (1 shorter events, 0.0 us)
Async XLA Ops:
  0.6 91.5 %copy-start.5 = (f32[4096]{0:T(1024)S(1)}, f32[4096]{0:T(1024)}, u32[]{:S(2)}) copy-start(f32[4096]{0:T(1024)} %param.22) | copy-start | bytes 49156
  44.6 2.2 %copy-start = (bf16[512,4096]{1,0:T(8,128)(2,1)S(1)}, bf16[512,4096]{1,0:T(8,128)(2,1)}, u32[]{:S(2)}) copy-start(bf16[512,4096]{1,0:T(8,128)(2,1)} %weight_ref.1) | copy-start | bytes 12582916
  46.8 0.9 copy-start.3
  47.8 0.9 copy-start.4
  48.7 43.4 %copy-start.1 = (bf16[4096,128]{1,0:T(8,128)(2,1)S(1)}, bf16[4096,128]{1,0:T(8,128)(2,1)}, u32[]{:S(2)}) copy-start(bf16[4096,128]{1,0:T(8,128)(2,1)} %wk_ref.1) | copy-start | bytes 3145732
  92.1 1.2 %copy-start.2 = (bf16[4096,128]{1,0:T(8,128)(2,1)S(1)}, bf16[4096,128]{1,0:T(8,128)(2,1)}, u32[]{:S(2)}) copy-start(bf16[4096,128]{1,0:T(8,128)(2,1)} %wv_ref.1) | copy-start | bytes 3145732
